TPU v7x, 32 devices: a whole 2x2x4 slice. The times are simulated.
32 devices in a mesh: il: 2 (over core), xl: 4 (over y, x), ta: 4 (over z).
Axes of the slice: x: 2, y: 2, z: 4, core: 2. Of those that a mesh axis runs over, the one named last changes fastest.
Arguments:
- traces: float32 [32, 832, 1024], P('il', 'xl', 'ta'), may hold values from -6 to 6
- bin_steps: int32 [2, 32, 832], P(None, 'il', 'xl'), may hold values from -1 to 1
Outputs:
- regridded: float32 [16, 416, 1536], P('il', 'xl', 'ta')
Inputs may be any that keep to these rules, and one draw needn't show every extreme that they name: `bin_steps`: every entry is -1, 0 or 1.
All inputs are finite; a program needn't handle non-finite values.
Results may differ from a plain program's by a relative error of at most 0.0001.
Values sent between devices are 32-bit elements; how exact they have to be, the bound alone decides.
A program may use at most 128 MiB of HBM per device.

v0:
```python
import jax
import jax.numpy as jnp
from jax import lax
from jax.sharding import PartitionSpec as P

TAPS = 16
P_SIZE = 3
Q = 2


def extended(shard, sides, width):
    for axis, dim in sides:
        devices, length = (lax.axis_size(axis), shard.shape[dim])
        up = [(i, (i + 1) % devices) for i in range(devices - 1)]
        down = [(j, i) for i, j in up]
        last = lax.slice_in_dim(shard, length - width, length, axis=dim)
        first = lax.slice_in_dim(shard, 0, width, axis=dim)
        before = lax.ppermute(last, axis, up)
        after = lax.ppermute(first, axis, down)
        shard = jnp.concatenate([before, shard, after], axis=dim)
    return shard


def shifted(shard, axis, by):
    devices = lax.axis_size(axis)
    pairs = [(i, i + by) for i in range(devices) if 0 <= i + by < devices]
    return lax.ppermute(shard, axis, pairs)


def lanczos_table(row_count, col_count, tap_reach, ratio_p, ratio_q):
    row_ids = lax.broadcasted_iota(jnp.int32, (row_count, col_count), 0)
    col_ids = lax.broadcasted_iota(jnp.int32, (row_count, col_count), 1)
    offset = (col_ids * ratio_q - (row_ids - tap_reach) * ratio_p).astype(
        jnp.float32
    ) / jnp.float32(ratio_p)
    inside = jnp.abs(offset) < jnp.float32(tap_reach)
    weights = jnp.sinc(offset) * jnp.sinc(offset / jnp.float32(tap_reach))
    return jnp.where(inside, weights, jnp.zeros_like(weights))


def widen_time(values, tap_reach):
    return extended(values, (("ta", 2),), tap_reach)


def resample(widened, tap_reach):
    row_count, col_count, length = widened.shape
    span = length - 2 * tap_reach
    block = 128
    count = span // block
    out_len = block * P_SIZE // Q
    taps_table = lanczos_table(block + 2 * tap_reach, out_len, tap_reach, P_SIZE, Q)
    flat_rows = widened.reshape(row_count * col_count, length)
    windows = jnp.stack(
        [flat_rows[:, k * block : k * block + block + 2 * tap_reach] for k in range(count)], axis=1
    )
    result = jnp.dot(
        windows, taps_table, precision=lax.Precision.HIGHEST, preferred_element_type=jnp.float32
    )
    return result.reshape(row_count, col_count, count * out_len)


def bin_sums(values, bin_steps):
    row_count, col_count, length = values.shape
    half_rows = row_count // 2
    half_cols = col_count // 2
    bin_total = jnp.zeros((half_rows + 2, half_cols + 2, length), jnp.float32)
    fold_count = jnp.zeros((half_rows + 2, half_cols + 2), jnp.float32)
    for row_phase in (0, 1):
        for col_phase in (0, 1):
            sub_values = values[row_phase::2, col_phase::2]
            step_il = bin_steps[0, row_phase::2, col_phase::2]
            step_xl = bin_steps[1, row_phase::2, col_phase::2]
            for shift_il in (-1, 0, 1):
                for shift_xl in (-1, 0, 1):
                    chosen = ((step_il == shift_il) & (step_xl == shift_xl)).astype(jnp.float32)
                    widths = ((1 + shift_il, 1 - shift_il), (1 + shift_xl, 1 - shift_xl))
                    bin_total = bin_total + jnp.pad(
                        sub_values * chosen[:, :, None], widths + ((0, 0),)
                    )
                    fold_count = fold_count + jnp.pad(chosen, widths)
    return (bin_total, fold_count)


def fold_rims(bin_total, fold_count):
    from_lower = shifted((bin_total[:, -1:], fold_count[:, -1:]), "xl", 1)
    from_upper = shifted((bin_total[:, :1], fold_count[:, :1]), "xl", -1)
    owned_sums = bin_total[:, 1:-1].at[:, :1].add(from_lower[0]).at[:, -1:].add(from_upper[0])
    owned_folds = fold_count[:, 1:-1].at[:, :1].add(from_lower[1]).at[:, -1:].add(from_upper[1])
    from_lower = shifted((owned_sums[-1:], owned_folds[-1:]), "il", 1)
    from_upper = shifted((owned_sums[:1], owned_folds[:1]), "il", -1)
    owned_sums = owned_sums[1:-1].at[:1].add(from_lower[0]).at[-1:].add(from_upper[0])
    owned_folds = owned_folds[1:-1].at[:1].add(from_lower[1]).at[-1:].add(from_upper[1])
    return (owned_sums, owned_folds)


def shards(traces, bin_steps):
    tap_reach = TAPS // 2
    bin_total, fold_count = bin_sums(traces, bin_steps)
    owned_sums, owned_folds = fold_rims(bin_total, fold_count)
    stacked = owned_sums / jnp.maximum(owned_folds, 1.0)[:, :, None]
    return resample(widen_time(stacked, tap_reach), tap_reach)


def solution(mesh):
    return jax.shard_map(
        shards,
        mesh=mesh,
        in_specs=(P("il", "xl", "ta"), P(None, "il", "xl")),
        out_specs=P("il", "xl", "ta"),
        check_vma=False,
    )
```

profile of v0, /device:TPU:4, one launch (start us, length us, event | category | flops | bytes accessed | tf_op | source)
XLA Modules:
  0.0 93.3 jit_solution(2392127374856807084)
XLA Ops:
  0.0 0.9 slice.261
  0.9 0.9 slice.262
  1.8 0.9 slice.264
  2.7 0.9 slice.265
  3.6 0.9 slice.267
  4.5 0.9 slice.268
  5.4 0.9 slice.270
  6.3 0.9 slice.271
  7.4 0.5 copy-done.4
  7.9 0.1 pad_add_fusion.1
  8.1 0.7 fusion.77
  8.7 3.5 %collective-permute-start.4 = (f32[10,1]{1,0:T(8,128)}, f32[10,1]{1,0:T(8,128)}, u32[]{:S(2)}, u32[]{:S(2)}) collective-permute-start(f32[10,1]{1,0:T(8,128)} %get-tuple-element.193), channel_id=1, source_target_pairs={{0,4},{4,8},{8,12},{1,5},{5,9},{9,13},{2,6},{6,10},{10,14},{3,7},{... | collective-permute-start | bytes 128 | tf_op jit(solution)/shard_map/ppermute | solution.py:27
  12.3 3.3 %collective-permute-start.5 = (f32[10,1]{1,0:T(8,128)}, f32[10,1]{1,0:T(8,128)}, u32[]{:S(2)}, u32[]{:S(2)}) collective-permute-start(f32[10,1]{1,0:T(8,128)} %get-tuple-element.192), channel_id=1, source_target_pairs={{4,0},{8,4},{12,8},{5,1},{9,5},{13,9},{6,2},{10,6},{14,10},{7,3},{... | collective-permute-start | bytes 128 | tf_op jit(solution)/shard_map/ppermute | solution.py:27
  15.6 5.6 %slice.260 = f32[8,104,256]{2,1,0:T(8,128)} slice(f32[16,208,256]{2,1,0:T(8,128)} %param.19), slice={[0:16:2], [0:208:2], [0:256:1]} | slice | bytes 1703936 | tf_op jit(solution)/shard_map/slice | solution.py:70
  21.2 5.6 %slice.263 = f32[8,104,256]{2,1,0:T(8,128)} slice(f32[16,208,256]{2,1,0:T(8,128)} %param.19), slice={[0:16:2], [1:208:2], [0:256:1]} | slice | bytes 1703936 | tf_op jit(solution)/shard_map/slice | solution.py:70
  26.8 3.3 %slice.266 = f32[8,104,256]{2,1,0:T(8,128)} slice(f32[16,208,256]{2,1,0:T(8,128)S(1)} %copy-done), slice={[1:16:2], [0:208:2], [0:256:1]} | slice | bytes 1703936 | tf_op jit(solution)/shard_map/slice | solution.py:70
  30.1 3.3 %slice.269 = f32[8,104,256]{2,1,0:T(8,128)} slice(f32[16,208,256]{2,1,0:T(8,128)S(1)} %copy-done), slice={[1:16:2], [1:208:2], [0:256:1]} | slice | bytes 1703936 | tf_op jit(solution)/shard_map/slice | solution.py:70
  33.4 2.3 %broadcast_multiply_fusion.35 = (f32[8,104,256]{2,1,0:T(8,128)S(1)}, f32[8,104,256]{2,1,0:T(8,128)S(1)}, f32[8,104,256]{2,1,0:T(8,128)S(1)}, f32[8,104,256]{2,1,...) fusion(f32[8,104,256]{2,1,0:T(8,128)} %slice.260, ...), kind=kLoop, calls=%fused_computation.42 | loop fusion | flops 1916928 | bytes 8549632 | tf_op jit(solution)/shard_map/mul | solution.py:78
  35.7 1.2 %broadcast_multiply_fusion.26 = (f32[8,104,256]{2,1,0:T(8,128)S(1)}, f32[8,104,256]{2,1,0:T(8,128)S(1)}, f32[8,104,256]{2,1,0:T(8,128)S(1)}, f32[8,104,256]{2,1,...) fusion(f32[8,104,256]{2,1,0:T(8,128)S(1)} %copy-done.3, ...), kind=kLoop, calls=%fused_computation.33 | loop fusion | flops 1916928 | bytes 8549632 | tf_op jit(solution)/shard_map/mul | solution.py:78
  37.0 2.8 %broadcast_multiply_fusion.17 = (f32[8,104,256]{2,1,0:T(8,128)S(1)}, f32[8,104,256]{2,1,0:T(8,128)S(1)}, f32[8,104,256]{2,1,0:T(8,128)S(1)}, f32[8,104,256]{2,1,...) fusion(f32[8,104,256]{2,1,0:T(8,128)S(1)} %copy-done.2, ...), kind=kLoop, calls=%fused_computation.24 | loop fusion | flops 1916928 | bytes 8549632 | tf_op jit(solution)/shard_map/mul | solution.py:78
  39.8 3.6 %broadcast_multiply_fusion.8 = (f32[8,104,256]{2,1,0:T(8,128)}, f32[8,104,256]{2,1,0:T(8,128)}, f32[8,104,256]{2,1,0:T(8,128)}, f32[8,104,256]{2,1,0:T(8,128)}, ...) fusion(f32[8,104,256]{2,1,0:T(8,128)S(1)} %copy-done.1, ...), kind=kLoop, calls=%fused_computation.15 | loop fusion | flops 1916928 | bytes 8549632 | tf_op jit(solution)/shard_map/mul | solution.py:78
  43.4 7.2 %pad_add_fusion = f32[10,106,256]{2,1,0:T(8,128)S(1)} fusion(f32[8,104,256]{2,1,0:T(8,128)} %get-tuple-element.182, f32[8,104,256]{2,1,0:T(8,128)} %get-tuple-element.183, f32[8,104,256]{2,1,0:T(8,128)} %get-tuple-element.184, f32[8,104,256]{2,1,0:T(8,128)} %get-tuple-element.185, f32[8,104,256]{2,1,0:T(8,128)} %get-tuple-element.186, ...), kind=kLoop, calls=%fused_computation.1 | loop fusion | flops 9497600 | bytes 31756288 | tf_op jit(solution)/shard_map/add | solution.py:77
  50.6 3.1 %collective-permute-start = (f32[10,1,256]{2,1,0:T(1,128)S(1)}, f32[10,1,256]{2,1,0:T(1,128)S(1)}, u32[]{:S(2)}, u32[]{:S(2)}) collective-permute-start(f32[10,1,256]{2,1,0:T(1,128)S(1)} %get-tuple-element.149), channel_id=1, source_target_pairs={{0,4},{4,8},{8,12},{1,5},{5,9},{9,13},{2,6},{6,10},{10,14},{3,7},{... | collective-permute-start | bytes 30728 | tf_op jit(solution)/shard_map/ppermute | solution.py:27
  53.7 3.7 %collective-permute-start.1 = (f32[10,1,256]{2,1,0:T(1,128)S(1)}, f32[10,1,256]{2,1,0:T(1,128)S(1)}, u32[]{:S(2)}, u32[]{:S(2)}) collective-permute-start(f32[10,1,256]{2,1,0:T(1,128)S(1)} %get-tuple-element.148), channel_id=1, source_target_pairs={{4,0},{8,4},{12,8},{5,1},{9,5},{13,9},{6,2},{10,6},{14,10},{7,3},{... | collective-permute-start | bytes 30728 | tf_op jit(solution)/shard_map/ppermute | solution.py:27
  57.4 0.6 compare_reduce_fusion
  58.1 1.4 %add_select_fusion = f32[10,1]{1,0:T(8,128)S(1)} fusion(f32[10,1]{1,0:T(8,128)} %collective-permute-done.4, f32[10,106]{1,0:T(8,128)S(1)} %pad_add_fusion.1, pred[]{:T(512)} %compare_reduce_fusion), kind=kLoop, calls=%fused_computation.117 | loop fusion | flops 20 | bytes 121 | tf_op jit(solution)/shard_map/select.12
  59.6 0.8 slice_add_fusion.4
  60.4 0.1 scatter-add.35
  60.4 1.3 %collective-permute-start.6 = (f32[1,104]{1,0:T(1,128)S(1)}, f32[1,104]{1,0:T(1,128)S(1)}, u32[]{:S(2)}, u32[]{:S(2)}) collective-permute-start(f32[1,104]{1,0:T(1,128)S(1)} %get-tuple-element.191), channel_id=1, source_target_pairs={{0,16},{1,17},{2,18},{3,19},{4,20},{5,21},{6,22},{7,23},{8,24},{9,... | collective-permute-start | bytes 1256 | tf_op jit(solution)/shard_map/ppermute | solution.py:27
  61.8 0.1 slice.296
  61.9 1.3 %collective-permute-start.7 = (f32[1,104]{1,0:T(1,128)S(1)}, f32[1,104]{1,0:T(1,128)S(1)}, u32[]{:S(2)}, u32[]{:S(2)}) collective-permute-start(f32[1,104]{1,0:T(1,128)S(1)} %get-tuple-element.190), channel_id=1, source_target_pairs={{16,0},{17,1},{18,2},{19,3},{20,4},{21,5},{22,6},{23,7},{24,8},{25... | collective-permute-start | bytes 1256 | tf_op jit(solution)/shard_map/ppermute | solution.py:27
  63.2 1.7 %collective-permute-done.7 = f32[1,104]{1,0:T(1,128)S(1)} collective-permute-done((f32[1,104]{1,0:T(1,128)S(1)}, f32[1,104]{1,0:T(1,128)S(1)}, u32[]{:S(2)}, u32[]{:S(2)}) %collective-permute-start.7) | collective-permute-done | bytes 448 | tf_op jit(solution)/shard_map/ppermute | solution.py:27
  65.2 2.1 %collective-permute-start.2 = (f32[1,104,256]{2,1,0:T(8,128)S(1)}, f32[1,104,256]{2,1,0:T(8,128)S(1)}, u32[]{:S(2)}, u32[]{:S(2)}) collective-permute-start(f32[1,104,256]{2,1,0:T(8,128)S(1)} %get-tuple-element.151), channel_id=1, source_target_pairs={{0,16},{1,17},{2,18},{3,19},{4,20},{5,21},{6,22},{7,23},{8,24},{9,... | collective-permute-start | bytes 319496 | tf_op jit(solution)/shard_map/ppermute | solution.py:27
  67.3 1.3 %collective-permute-start.3 = (f32[1,104,256]{2,1,0:T(8,128)S(1)}, f32[1,104,256]{2,1,0:T(8,128)S(1)}, u32[]{:S(2)}, u32[]{:S(2)}) collective-permute-start(f32[1,104,256]{2,1,0:T(8,128)S(1)} %get-tuple-element.150), channel_id=1, source_target_pairs={{16,0},{17,1},{18,2},{19,3},{20,4},{21,5},{22,6},{23,7},{24,8},{25... | collective-permute-start | bytes 319496 | tf_op jit(solution)/shard_map/ppermute | solution.py:27
  68.7 1.9 %collective-permute-done.3 = f32[1,104,256]{2,1,0:T(8,128)S(1)} collective-permute-done((f32[1,104,256]{2,1,0:T(8,128)S(1)}, f32[1,104,256]{2,1,0:T(8,128)S(1)}, u32[]{:S(2)}, u32[]{:S(2)}) %collective-permute-start.3) | collective-permute-done | bytes 106528 | tf_op jit(solution)/shard_map/ppermute | solution.py:27
  70.6 0.2 broadcast_divide_fusion
  70.8 0.2 fusion.75
  70.9 3.5 %collective-permute-start.8 = (f32[8,104,8]{2,1,0:T(8,128)S(1)}, f32[8,104,8]{2,1,0:T(8,128)S(1)}, u32[]{:S(2)}, u32[]{:S(2)}) collective-permute-start(f32[8,104,8]{2,1,0:T(8,128)S(1)} %get-tuple-element.152), channel_id=1, source_target_pairs={{0,1},{1,2},{2,3},{4,5},{5,6},{6,7},{8,9},{9,10},{10,11},{12,13},{... | collective-permute-start | bytes 79880 | tf_op jit(solution)/shard_map/ppermute | solution.py:18
  74.5 1.3 %collective-permute-start.9 = (f32[8,104,8]{2,1,0:T(8,128)S(1)}, f32[8,104,8]{2,1,0:T(8,128)S(1)}, u32[]{:S(2)}, u32[]{:S(2)}) collective-permute-start(f32[8,104,8]{2,1,0:T(8,128)S(1)} %get-tuple-element.153), channel_id=1, source_target_pairs={{1,0},{2,1},{3,2},{5,4},{6,5},{7,6},{9,8},{10,9},{11,10},{13,12},{... | collective-permute-start | bytes 79880 | tf_op jit(solution)/shard_map/ppermute | solution.py:19
  75.8 8.0 %collective-permute-done.8 = f32[8,104,8]{2,1,0:T(8,128)S(1)} collective-permute-done((f32[8,104,8]{2,1,0:T(8,128)S(1)}, f32[8,104,8]{2,1,0:T(8,128)S(1)}, u32[]{:S(2)}, u32[]{:S(2)}) %collective-permute-start.8) | collective-permute-done | bytes 26656 | tf_op jit(solution)/shard_map/ppermute | solution.py:18
  83.8 4.1 %collective-permute-done.9 = f32[8,104,8]{2,1,0:T(8,128)S(1)} collective-permute-done((f32[8,104,8]{2,1,0:T(8,128)S(1)}, f32[8,104,8]{2,1,0:T(8,128)S(1)}, u32[]{:S(2)}, u32[]{:S(2)}) %collective-permute-start.9) | collective-permute-done | bytes 26656 | tf_op jit(solution)/shard_map/ppermute | solution.py:19
  87.9 0.5 pad_maximum_fusion
  88.4 0.1 fusion.72
  88.6 0.3 copy.8
  88.8 0.3 copy.9
  89.1 1.8 %fusion = f32[832,2,192]{0,2,1:T(8,128)S(1)} fusion(f32[832,1,144]{0,2,1:T(8,128)S(1)} %bitcast.82, f32[832,1,144]{0,2,1:T(8,128)S(1)} %bitcast.81, s32[144]{0:T(256)S(1)} %add_multiply_fusion, s32[192]{0:T(256)S(1)} %iota_multiply_fusion), kind=kOutput, calls=%fused_computation.2 | convolution fusion | flops 554333184 | bytes 2237760 | tf_op jit(solution)/shard_map/dot_general | solution.py:56
  90.9 0.8 reshape.710
  91.7 1.6 %copy.6 = f32[8,104,384]{2,1,0:T(8,128)} copy(f32[8,104,384]{1,0,2:T(8,128)S(1)} %reshape.710) | data formatting | bytes 2555904 | tf_op jit(solution)/shard_map/reshape | solution.py:59
  (49 shorter events, 0.6 us)
Async XLA Ops:
  7.3 0.6 copy-start.4
  7.4 0.7 copy-start.5
  7.9 18.9 %copy-start = (f32[16,208,256]{2,1,0:T(8,128)S(1)}, f32[16,208,256]{2,1,0:T(8,128)}, u32[]{:S(2)}) copy-start(f32[16,208,256]{2,1,0:T(8,128)} %param.19) | copy-start | bytes 10223620
  8.7 49.4 %collective-permute-start.4 = (f32[10,1]{1,0:T(8,128)}, f32[10,1]{1,0:T(8,128)}, u32[]{:S(2)}, u32[]{:S(2)}) collective-permute-start(f32[10,1]{1,0:T(8,128)} %get-tuple-element.193), channel_id=1, source_target_pairs={{0,4},{4,8},{8,12},{1,5},{5,9},{9,13},{2,6},{6,10},{10,14},{3,7},{... | collective-permute-start | bytes 128 | tf_op jit(solution)/shard_map/ppermute | solution.py:27
  12.3 47.3 %collective-permute-start.5 = (f32[10,1]{1,0:T(8,128)}, f32[10,1]{1,0:T(8,128)}, u32[]{:S(2)}, u32[]{:S(2)}) collective-permute-start(f32[10,1]{1,0:T(8,128)} %get-tuple-element.192), channel_id=1, source_target_pairs={{4,0},{8,4},{12,8},{5,1},{9,5},{13,9},{6,2},{10,6},{14,10},{7,3},{... | collective-permute-start | bytes 128 | tf_op jit(solution)/shard_map/ppermute | solution.py:27
  33.4 2.3 %copy-start.3 = (f32[8,104,256]{2,1,0:T(8,128)S(1)}, f32[8,104,256]{2,1,0:T(8,128)}, u32[]{:S(2)}) copy-start(f32[8,104,256]{2,1,0:T(8,128)} %slice.263) | copy-start | bytes 2555908
  35.7 1.2 %copy-start.2 = (f32[8,104,256]{2,1,0:T(8,128)S(1)}, f32[8,104,256]{2,1,0:T(8,128)}, u32[]{:S(2)}) copy-start(f32[8,104,256]{2,1,0:T(8,128)} %slice.266) | copy-start | bytes 2555908
  37.0 2.8 %copy-start.1 = (f32[8,104,256]{2,1,0:T(8,128)S(1)}, f32[8,104,256]{2,1,0:T(8,128)}, u32[]{:S(2)}) copy-start(f32[8,104,256]{2,1,0:T(8,128)} %slice.269) | copy-start | bytes 2555908
  50.6 14.3 %collective-permute-start = (f32[10,1,256]{2,1,0:T(1,128)S(1)}, f32[10,1,256]{2,1,0:T(1,128)S(1)}, u32[]{:S(2)}, u32[]{:S(2)}) collective-permute-start(f32[10,1,256]{2,1,0:T(1,128)S(1)} %get-tuple-element.149), channel_id=1, source_target_pairs={{0,4},{4,8},{8,12},{1,5},{5,9},{9,13},{2,6},{6,10},{10,14},{3,7},{... | collective-permute-start | bytes 30728 | tf_op jit(solution)/shard_map/ppermute | solution.py:27
  53.7 11.3 %collective-permute-start.1 = (f32[10,1,256]{2,1,0:T(1,128)S(1)}, f32[10,1,256]{2,1,0:T(1,128)S(1)}, u32[]{:S(2)}, u32[]{:S(2)}) collective-permute-start(f32[10,1,256]{2,1,0:T(1,128)S(1)} %get-tuple-element.148), channel_id=1, source_target_pairs={{4,0},{8,4},{12,8},{5,1},{9,5},{13,9},{6,2},{10,6},{14,10},{7,3},{... | collective-permute-start | bytes 30728 | tf_op jit(solution)/shard_map/ppermute | solution.py:27
  60.4 2.7 %collective-permute-start.6 = (f32[1,104]{1,0:T(1,128)S(1)}, f32[1,104]{1,0:T(1,128)S(1)}, u32[]{:S(2)}, u32[]{:S(2)}) collective-permute-start(f32[1,104]{1,0:T(1,128)S(1)} %get-tuple-element.191), channel_id=1, source_target_pairs={{0,16},{1,17},{2,18},{3,19},{4,20},{5,21},{6,22},{7,23},{8,24},{9,... | collective-permute-start | bytes 1256 | tf_op jit(solution)/shard_map/ppermute | solution.py:27
  61.9 3.1 %collective-permute-start.7 = (f32[1,104]{1,0:T(1,128)S(1)}, f32[1,104]{1,0:T(1,128)S(1)}, u32[]{:S(2)}, u32[]{:S(2)}) collective-permute-start(f32[1,104]{1,0:T(1,128)S(1)} %get-tuple-element.190), channel_id=1, source_target_pairs={{16,0},{17,1},{18,2},{19,3},{20,4},{21,5},{22,6},{23,7},{24,8},{25... | collective-permute-start | bytes 1256 | tf_op jit(solution)/shard_map/ppermute | solution.py:27
  65.2 3.5 %collective-permute-start.2 = (f32[1,104,256]{2,1,0:T(8,128)S(1)}, f32[1,104,256]{2,1,0:T(8,128)S(1)}, u32[]{:S(2)}, u32[]{:S(2)}) collective-permute-start(f32[1,104,256]{2,1,0:T(8,128)S(1)} %get-tuple-element.151), channel_id=1, source_target_pairs={{0,16},{1,17},{2,18},{3,19},{4,20},{5,21},{6,22},{7,23},{8,24},{9,... | collective-permute-start | bytes 319496 | tf_op jit(solution)/shard_map/ppermute | solution.py:27
  67.3 3.2 %collective-permute-start.3 = (f32[1,104,256]{2,1,0:T(8,128)S(1)}, f32[1,104,256]{2,1,0:T(8,128)S(1)}, u32[]{:S(2)}, u32[]{:S(2)}) collective-permute-start(f32[1,104,256]{2,1,0:T(8,128)S(1)} %get-tuple-element.150), channel_id=1, source_target_pairs={{16,0},{17,1},{18,2},{19,3},{20,4},{21,5},{22,6},{23,7},{24,8},{25... | collective-permute-start | bytes 319496 | tf_op jit(solution)/shard_map/ppermute | solution.py:27
  70.9 12.9 %collective-permute-start.8 = (f32[8,104,8]{2,1,0:T(8,128)S(1)}, f32[8,104,8]{2,1,0:T(8,128)S(1)}, u32[]{:S(2)}, u32[]{:S(2)}) collective-permute-start(f32[8,104,8]{2,1,0:T(8,128)S(1)} %get-tuple-element.152), channel_id=1, source_target_pairs={{0,1},{1,2},{2,3},{4,5},{5,6},{6,7},{8,9},{9,10},{10,11},{12,13},{... | collective-permute-start | bytes 79880 | tf_op jit(solution)/shard_map/ppermute | solution.py:18
  74.5 13.5 %collective-permute-start.9 = (f32[8,104,8]{2,1,0:T(8,128)S(1)}, f32[8,104,8]{2,1,0:T(8,128)S(1)}, u32[]{:S(2)}, u32[]{:S(2)}) collective-permute-start(f32[8,104,8]{2,1,0:T(8,128)S(1)} %get-tuple-element.153), channel_id=1, source_target_pairs={{1,0},{2,1},{3,2},{5,4},{6,5},{7,6},{9,8},{10,9},{11,10},{13,12},{... | collective-permute-start | bytes 79880 | tf_op jit(solution)/shard_map/ppermute | solution.py:19
where the time goes:
time: 94.4 us; the launch traced here: 93.3 us
  local copies, waits for them, and re-layouts  30 us (32%)
  starting transfers between devices  24.4 us (26%)
  other arithmetic  20.9 us (22%)
  waiting for transfers between devices  15.8 us (17%)
  matrix products  1.78 us (2%)
    ppermute x8, starting transfers between devices, shifted(): return lax.ppermute(shard, axis, pairs)  19.6 us
    slice x4, local copies, waits for them, and re-layouts, bin_sums(): sub_values = values[row_phase::2, col_phase::2]  17.8 us
    mul x4, other arithmetic, bin_sums(): sub_values * chosen[:, :, None]  9.91 us
    ppermute x1, waiting for transfers between devices, extended(): before = lax.ppermute(last, axis, up)  8.04 us
    add x1, other arithmetic, bin_sums(): bin_total + jnp.pad(sub_values * chosen[:, :, None], widths + ((0, 0),))  7.18 us
    ppermute x1, waiting for transfers between devices, extended(): after = lax.ppermute(first, axis, down)  4.14 us
    slice x4, local copies, waits for them, and re-layouts, bin_sums(): step_xl = bin_steps[1, row_phase::2, col_phase::2]  3.59 us
    ppermute x8, waiting for transfers between devices, shifted(): return lax.ppermute(shard, axis, pairs)  3.59 us
  transfers between devices with their start and end apart: 10, of which 4 were waited for; matrix products, arithmetic and copies ran while one was open for 41% of the time, Pallas kernels for 0%

commit v1 on v0

v1 whole, which is shorter than its diff:
```python
import functools

import numpy as np
import jax
import jax.numpy as jnp
from jax import lax
from jax.experimental import pallas as pl
from jax.experimental.pallas import tpu as pltpu
from jax.sharding import PartitionSpec as P

TAPS = 16
P_SIZE = 3
Q = 2
MESH = pl.DeviceIdType.MESH
F32, BF16 = jnp.float32, jnp.bfloat16


def lanczos_table(span):
    reach = TAPS // 2
    rows = np.arange(span + 2 * reach)[:, None] - reach
    cols = np.arange(span * P_SIZE // Q)[None, :]
    offset = (cols * Q - rows * P_SIZE).astype(np.float64) / P_SIZE
    weights = np.sinc(offset) * np.sinc(offset / reach)
    return np.where(np.abs(offset) < reach, weights, 0.0).astype(np.float32)


def split_table(table):
    high = table.astype(BF16)
    low = (table - high.astype(np.float32)).astype(BF16)
    return high, low


def halves(values):
    high = values.astype(BF16)
    low = (values - high.astype(F32)).astype(BF16)
    return high, low


def dot(a, b):
    return jnp.dot(a, b, preferred_element_type=F32)


def kernel(n_xl, n_ta, traces, steps, t_high, t_low, t_edge, out, x, acc, rim_send, rim_recv,
           il_recv, corner_recv, halo_send, halo_recv, load_sem, send_sem, recv_sem):
    n_rows, n_cols, span = x.shape
    n_pairs = n_rows // 2
    own_cols = n_cols // 2
    reach = TAPS // 2
    il, xl, ta = lax.axis_index("il"), lax.axis_index("xl"), lax.axis_index("ta")
    other = 1 - il
    xl_up, xl_down = lax.rem(xl + 1, n_xl), lax.rem(xl + n_xl - 1, n_xl)
    ta_up, ta_down = lax.rem(ta + 1, n_ta), lax.rem(ta + n_ta - 1, n_ta)

    loads = []
    for p in range(n_pairs):
        load = pltpu.make_async_copy(traces.at[pl.ds(2 * p, 2)], x.at[pl.ds(2 * p, 2)], load_sem.at[p])
        load.start()
        loads.append(load)
    barrier = pltpu.get_barrier_semaphore()
    partners = ({"il": other}, {"xl": xl_up}, {"xl": xl_down}, {"il": other, "xl": xl_up},
                {"il": other, "xl": xl_down}, {"ta": ta_up}, {"ta": ta_down})
    for partner in partners:
        pl.semaphore_signal(barrier, inc=1, device_id=partner, device_id_type=MESH)

    split = own_cols // 16 * 16
    if split == n_cols or split < 16:
        raise ValueError("column count")
    ranges = []
    for start, stop in ((0, split), (split, n_cols)):
        first = start // 2 // 8 * 8
        last = (stop - 1) // 2 + 2
        ranges.append((start, stop, first, (last + 1 - first + 7) // 8 * 8))
    col = lax.broadcasted_iota(jnp.int32, (n_rows, n_cols), 1)
    bin_col = lax.shift_right_logical(col, 1) + steps[1] + 1
    bin_row = steps[0] + 1
    acc[...] = jnp.zeros_like(acc)
    codes = [bin_row * height + bin_col - first for _, _, first, height in ranges]
    for p in range(n_pairs):
        loads[p].wait()
        for (start, stop, first, height), code in zip(ranges, codes):
            depth = 2 * (stop - start)
            key = jnp.concatenate([code[2 * p: 2 * p + 1, start:stop], code[2 * p + 1: 2 * p + 2, start:stop]], axis=1)
            rows = lax.broadcasted_iota(jnp.int32, (3 * height, depth), 0)
            chosen = jnp.where(rows == key, 1.0, 0.0).astype(BF16)
            values = jnp.concatenate([x[2 * p, start:stop, :], x[2 * p + 1, start:stop, :]], axis=0)
            high, low = halves(values)
            sums = dot(chosen, high) + dot(chosen, low)
            folds = dot(chosen, jnp.ones((depth, 128), BF16))
            for r in range(3):
                acc[p + r, first: first + height, :span] += sums[r * height: (r + 1) * height]
                acc[p + r, first: first + height, span:] += folds[r * height: (r + 1) * height]

    rim_row = jnp.where(il == 0, n_pairs + 1, 0)
    own_row = jnp.where(il == 0, n_pairs, 1)
    pl.semaphore_wait(barrier, len(partners))

    def send(src, dst, slot, partner):
        copy = pltpu.make_async_remote_copy(src_ref=src, dst_ref=dst, send_sem=send_sem.at[slot],
                                            recv_sem=recv_sem.at[slot], device_id=partner, device_id_type=MESH)
        copy.start()
        return copy

    copies = [send(acc.at[rim_row], il_recv, 0, {"il": other})]
    for r in range(n_pairs + 2):
        rim_send[0, r] = acc[r, own_cols + 1: own_cols + 2, :]
        rim_send[1, r] = acc[r, 0:1, :]
    for d, where in ((0, xl_up), (1, xl_down)):
        copies.append(send(rim_send.at[d], rim_recv.at[d], 1 + d, {"xl": where}))
        copies.append(send(rim_send.at[d, rim_row], corner_recv.at[d], 3 + d, {"il": other, "xl": where}))
    for copy in copies:
        copy.wait()
    acc[own_row] = acc[own_row] + il_recv[...]
    for d, (column, real) in enumerate(((1, xl > 0), (own_cols, xl < n_xl - 1))):
        for r in range(1, n_pairs + 1):
            acc[r, column: column + 1, :] += jnp.where(real, rim_recv[d, r], 0.0)
        acc[own_row, column: column + 1, :] += jnp.where(real, corner_recv[d], 0.0)

    for b in range(n_pairs):
        lanes = slice(b * 128, b * 128 + own_cols)
        halo_send[0, :, lanes] = acc[b + 1, 1: own_cols + 1, :128].T[:reach]
        halo_send[1, :, lanes] = acc[b + 1, 1: own_cols + 1, span - 128: span].T[128 - reach:]
    halos = [send(halo_send.at[1], halo_recv.at[0], 5, {"ta": ta_up}),
             send(halo_send.at[0], halo_recv.at[1], 6, {"ta": ta_down})]
    for b in range(n_pairs):
        high, low = halves(acc[b + 1, 1: own_cols + 1, :span])
        out[b] = dot(high, t_high[...]) + (dot(low, t_high[...]) + dot(high, t_low[...]))
    for copy in halos:
        copy.wait()
    for b in range(n_pairs):
        lanes = slice(b * 128, (b + 1) * 128)
        before = jnp.where(ta > 0, halo_recv[0, :, lanes], 0.0)
        after = jnp.where(ta < n_ta - 1, halo_recv[1, :, lanes], 0.0)
        edges = jnp.concatenate([before, after], axis=0).T[:own_cols]
        high, low = halves(edges)
        edge_high, edge_low = t_edge[0], t_edge[1]
        edge = dot(high, edge_high) + (dot(low, edge_high) + dot(high, edge_low))
        scale = 1.0 / jnp.maximum(acc[b + 1, 1: own_cols + 1, span:], 1.0)
        out[b] = (out[b] + edge) * jnp.concatenate([scale] * (edge.shape[1] // 128), axis=1)


def shards(n_xl, n_ta, traces, bin_steps):
    n_rows, n_cols, span = traces.shape
    n_pairs, own_cols = n_rows // 2, n_cols // 2
    reach = TAPS // 2
    padded = (own_cols + 2 + 7) // 8 * 8
    width = span + 128
    out_span = span * P_SIZE // Q
    table = lanczos_table(span)
    t_high, t_low = split_table(table[reach:-reach])
    t_edge = np.stack(split_table(np.concatenate([table[:reach], table[-reach:]])))
    vmem = pl.BlockSpec(memory_space=pltpu.VMEM)
    return pl.pallas_call(
        functools.partial(kernel, n_xl, n_ta),
        out_shape=jax.ShapeDtypeStruct((n_pairs, own_cols, out_span), F32),
        in_specs=[pl.BlockSpec(memory_space=pl.ANY)] + [vmem] * 4,
        out_specs=vmem,
        scratch_shapes=[
            pltpu.VMEM((n_rows, n_cols, span), F32),
            pltpu.VMEM((n_pairs + 2, padded, width), F32),
            pltpu.VMEM((2, n_pairs + 2, 1, width), F32),
            pltpu.VMEM((2, n_pairs + 2, 1, width), F32),
            pltpu.VMEM((padded, width), F32),
            pltpu.VMEM((2, 1, width), F32),
            pltpu.VMEM((2, reach, n_pairs * 128), F32),
            pltpu.VMEM((2, reach, n_pairs * 128), F32),
            pltpu.SemaphoreType.DMA((n_pairs,)),
            pltpu.SemaphoreType.DMA((7,)),
            pltpu.SemaphoreType.DMA((7,)),
        ],
        compiler_params=pltpu.CompilerParams(collective_id=0, has_side_effects=True),
    )(traces, bin_steps, jnp.asarray(t_high), jnp.asarray(t_low), jnp.asarray(t_edge))


def solution(mesh):
    if mesh.shape["il"] != 2:
        raise ValueError("il size")
    return jax.shard_map(
        functools.partial(shards, mesh.shape["xl"], mesh.shape["ta"]),
        mesh=mesh,
        in_specs=(P("il", "xl", "ta"), P(None, "il", "xl")),
        out_specs=P("il", "xl", "ta"),
        check_vma=False,
    )
```

time: 94.4 us -> 20.9 us (0.22)
  the two profiles are of different devices: /device:TPU:4 before, /device:TPU:0 now
where the time goes in v1:
time: 20.9 us; the launch traced here: 20.7 us
  Pallas kernels  18.3 us (88%)
  local copies, waits for them, and re-layouts  2.43 us (12%)
    pallas_call x1, Pallas kernels, shards(): pl.pallas_call(functools.partial(kernel, n_xl, n_ta), out_shape=jax.Shape...  18.3 us
    unnamed x1, local copies, waits for them, and re-layouts  2.43 us

profile of v1, /device:TPU:0, one launch (start us, length us, event | category | flops | bytes accessed | tf_op | source)
XLA Modules:
  0.0 20.7 jit_solution(15801840779522937898)
XLA Ops:
  0.0 18.3 %shard_map.55 = f32[8,104,384]{2,1,0:T(8,128)} custom-call(f32[16,208,256]{2,1,0:T(8,128)} %traces.1, s32[2,16,208]{2,1,0:T(8,128)} %steps.1, bf16[256,384]{1,0:T(8,128)(2,1)} %constant.6.clone.t_high, bf16[256,384]{1,0:T(8,128)(2,1)} %constant.7.clone.t_low, bf16[2,16,384]{2,1,0:T(8,128)(2,1)} %constant.8.clone.t_edge), custom_call_target="tpu_custom_call" | custom-call | tf_op jit(solution)/shard_map/pallas_call | solution.py:152
  18.3 2.4 %copy.7 = f32[8,104,384]{2,1,0:T(8,128)} copy(f32[8,104,384]{2,1,0:T(8,128)} %shard_map.55) | data formatting | bytes 2555904

commit v2 on v1

v2 whole, which is shorter than its diff:
```python
import functools

import numpy as np
import jax
import jax.numpy as jnp
from jax import lax
from jax.experimental import pallas as pl
from jax.experimental.pallas import tpu as pltpu
from jax.sharding import PartitionSpec as P

TAPS = 16
P_SIZE = 3
Q = 2
MESH = pl.DeviceIdType.MESH
F32, BF16 = jnp.float32, jnp.bfloat16


def lanczos_table(span):
    reach = TAPS // 2
    rows = np.arange(span + 2 * reach)[:, None] - reach
    cols = np.arange(span * P_SIZE // Q)[None, :]
    offset = (cols * Q - rows * P_SIZE).astype(np.float64) / P_SIZE
    weights = np.sinc(offset) * np.sinc(offset / reach)
    return np.where(np.abs(offset) < reach, weights, 0.0).astype(np.float32)


def split_table(table):
    high = table.astype(BF16)
    low = (table - high.astype(np.float32)).astype(BF16)
    return high, low


def halves(values):
    high = values.astype(BF16)
    low = (values - high.astype(F32)).astype(BF16)
    return high, low


def dot(a, b):
    return jnp.dot(a, b, preferred_element_type=F32)


def column_ranges(n_cols):
    split = n_cols // 2 // 16 * 16
    if split < 16 or n_cols % 16:
        raise ValueError("column count")
    ranges = []
    for start, stop in ((0, split), (split, n_cols)):
        first = start // 2 // 8 * 8
        last = (stop - 1) // 2 + 2
        ranges.append((start, stop, first, (last + 1 - first + 7) // 8 * 8))
    return ranges


def binning(n_xl, n_ta, traces, steps_hbm, t_high_hbm, t_low_hbm, main, scale, halo_out, x, edge_x, steps, t_high, t_low, keys,
            acc, rim_send, rim_recv, il_recv, corner_recv, halo_send, halo_recv, load_sem, edge_sem, table_sem,
            send_sem, recv_sem):
    n_rows, n_cols, span = x.shape
    n_pairs = n_rows // 2
    own_cols = n_cols // 2
    reach = TAPS // 2
    il, xl, ta = lax.axis_index("il"), lax.axis_index("xl"), lax.axis_index("ta")
    other = 1 - il
    has_xl = (xl < n_xl - 1, xl > 0)
    has_ta = (ta < n_ta - 1, ta > 0)
    xl_at, ta_at = (xl + 1, xl - 1), (ta + 1, ta - 1)

    def when(condition, work):
        pl.when(condition)(work)

    def pair(p):
        return jnp.where(il == 0, n_pairs - 1 - p, p)

    step_load = pltpu.make_async_copy(steps_hbm, steps, table_sem.at[2])
    step_load.start()
    edge_loads = [pltpu.make_async_copy(traces.at[:, pl.ds(start, 8)], edge_x.at[d], edge_sem.at[d])
                  for d, start in enumerate((n_cols - 8, 0))]
    for load in edge_loads:
        load.start()
    loads = []
    for p in range(n_pairs):
        rows = pl.ds(2 * pair(p), 2)
        loads.append(pltpu.make_async_copy(traces.at[rows], x.at[rows], load_sem.at[p]))
    for load in loads:
        load.start()
    table_loads = [pltpu.make_async_copy(t_high_hbm, t_high, table_sem.at[0]),
                   pltpu.make_async_copy(t_low_hbm, t_low, table_sem.at[1])]
    for load in table_loads:
        load.start()

    barrier = pltpu.get_barrier_semaphore()

    def greet(partner):
        pl.semaphore_signal(barrier, inc=1, device_id=partner, device_id_type=MESH)

    greet({"il": other})
    for d in range(2):
        def both(d=d):
            greet({"xl": xl_at[d]})
            greet({"il": other, "xl": xl_at[d]})
        when(has_xl[d], both)
        when(has_ta[d], lambda d=d: greet({"ta": ta_at[d]}))

    acc[...] = jnp.zeros_like(acc)
    step_load.wait()
    ranges = column_ranges(n_cols)
    col = lax.broadcasted_iota(jnp.int32, (n_rows, n_cols), 1)
    bin_col = lax.shift_right_logical(col, 1) + steps[1] + 1
    bin_row = steps[0] + 1
    for k, (start, stop, first, height) in enumerate(ranges):
        code = bin_row * height + bin_col - first
        for p in range(n_pairs):
            keys[k, p, :, :2 * (stop - start)] = jnp.concatenate(
                [code[2 * p: 2 * p + 1, start:stop], code[2 * p + 1: 2 * p + 2, start:stop]], axis=1)

    def one_hot(key, height):
        rows = lax.broadcasted_iota(jnp.int32, (height, key.shape[1]), 0)
        return jnp.where(rows == key, 1.0, 0.0).astype(BF16)

    def totals(chosen, values):
        high, low = halves(values)
        return (dot(chosen, high) + dot(chosen, low), dot(chosen, jnp.ones((values.shape[0], 128), BF16)))

    def bin_pair(p):
        at = pair(p)
        loads[p].wait()
        for k, (start, stop, first, height) in enumerate(ranges):
            key = keys[k, at][:, :2 * (stop - start)]
            values = jnp.concatenate([x[2 * at, start:stop, :], x[2 * at + 1, start:stop, :]], axis=0)
            sums, folds = totals(one_hot(key, 3 * height), values)
            for r in range(3):
                acc[at + r, first: first + height, :span] += sums[r * height: (r + 1) * height]
                acc[at + r, first: first + height, span:] += folds[r * height: (r + 1) * height]

    def remote(src, dst, slot, partner):
        return pltpu.make_async_remote_copy(src_ref=src, dst_ref=dst, send_sem=send_sem.at[slot],
                                            recv_sem=recv_sem.at[slot], device_id=partner, device_id_type=MESH)

    rim_row = jnp.where(il == 0, n_pairs + 1, 0)
    own_row = jnp.where(il == 0, n_pairs, 1)
    to_other = remote(acc.at[rim_row], il_recv, 0, {"il": other})
    rims = [(remote(rim_send.at[d], rim_recv.at[d], 1 + d, {"xl": xl_at[d]}),
             remote(rim_send.at[d, rim_row], corner_recv.at[d], 3 + d, {"il": other, "xl": xl_at[d]}))
            for d in range(2)]

    row = lax.broadcasted_iota(jnp.int32, (n_rows, n_cols), 0)
    rim_bin = bin_row + lax.shift_right_logical(row, 1)
    for load in edge_loads:
        load.wait()
    for d, (start, column) in enumerate(((n_cols - 8, own_cols + 1), (0, 0))):
        target = jnp.where(bin_col == column, rim_bin, -1)
        key = jnp.concatenate([target[i: i + 1, start: start + 8] for i in range(n_rows)], axis=1)
        sums, folds = totals(one_hot(key, (n_pairs + 2 + 7) // 8 * 8), edge_x[d].reshape(n_rows * 8, span))
        for r in range(n_pairs + 2):
            rim_send[d, r, :, :span] = sums[r: r + 1]
            rim_send[d, r, :, span:] = folds[r: r + 1]
    bin_pair(0)
    peers = 1
    for d in range(2):
        peers = peers + jnp.where(has_xl[d], 2, 0) + jnp.where(has_ta[d], 1, 0)
    pl.semaphore_wait(barrier, peers)
    to_other.start()
    for d in range(2):
        def go(d=d):
            for copy in rims[d]:
                copy.start()
        when(has_xl[d], go)
    for p in range(1, n_pairs):
        bin_pair(p)
    to_other.wait_recv()
    acc[own_row] = acc[own_row] + il_recv[...]
    for d, column in enumerate((1, own_cols)):
        def add(d=d, column=column):
            for copy in rims[d]:
                copy.wait_recv()
            for r in range(1, n_pairs + 1):
                acc[r, column: column + 1, :] += rim_recv[d, r]
            acc[own_row, column: column + 1, :] += corner_recv[d]
        when(has_xl[1 - d], add)

    halos = [remote(halo_send.at[d], halo_recv.at[d], 5 + d, {"ta": ta_at[d]}) for d in range(2)]
    for b in range(n_pairs):
        lanes = slice(b * 128, b * 128 + own_cols)
        halo_send[0, :, lanes] = acc[b + 1, 1: own_cols + 1, span - 128: span].T[128 - reach:]
        halo_send[1, :, lanes] = acc[b + 1, 1: own_cols + 1, :128].T[:reach]
    for d in range(2):
        when(has_ta[d], halos[d].start)
    for load in table_loads:
        load.wait()
    for b in range(n_pairs):
        high, low = halves(acc[b + 1, 1: own_cols + 1, :span])
        main[b] = dot(high, t_high[...]) + (dot(low, t_high[...]) + dot(high, t_low[...]))
        scale[b] = 1.0 / jnp.maximum(acc[b + 1, 1: own_cols + 1, span:], 1.0)
    for d in range(2):
        def arrived(d=d):
            halos[d].wait_recv()
            halo_out[d] = halo_recv[d]

        def absent(d=d):
            halo_out[d] = jnp.zeros_like(halo_recv[d])
        when(has_ta[1 - d], arrived)
        when(jnp.logical_not(has_ta[1 - d]), absent)
    for d in range(2):
        when(has_ta[d], halos[d].wait_send)
        def sent(d=d):
            for copy in rims[d]:
                copy.wait_send()
        when(has_xl[d], sent)
    to_other.wait_send()


def finish(main, scale, halo, t_edge, out, staged, out_sem):
    n_pairs, own_cols, width = main.shape
    writes = []
    for b in range(n_pairs):
        lanes = slice(b * 128, (b + 1) * 128)
        edges = jnp.concatenate([halo[0, :, lanes], halo[1, :, lanes]], axis=0).T[:own_cols]
        high, low = halves(edges)
        edge = dot(high, t_edge[0]) + (dot(low, t_edge[0]) + dot(high, t_edge[1]))
        staged[b] = (main[b] + edge) * jnp.concatenate([scale[b]] * (width // 128), axis=1)
        write = pltpu.make_async_copy(staged.at[b], out.at[b], out_sem.at[b])
        write.start()
        writes.append(write)
    for write in writes:
        write.wait()


def shards(n_xl, n_ta, traces, bin_steps):
    n_rows, n_cols, span = traces.shape
    n_pairs, own_cols = n_rows // 2, n_cols // 2
    reach = TAPS // 2
    padded = (own_cols + 2 + 7) // 8 * 8
    width = span + 128
    out_span = span * P_SIZE // Q
    table = lanczos_table(span)
    t_high, t_low = split_table(table[reach:-reach])
    t_edge = np.stack(split_table(np.concatenate([table[:reach], table[-reach:]])))
    vmem = pl.BlockSpec(memory_space=pltpu.VMEM)
    hbm = pl.BlockSpec(memory_space=pltpu.HBM)
    main, scale, halo = pl.pallas_call(
        functools.partial(binning, n_xl, n_ta),
        out_shape=(pltpu.VMEM((n_pairs, own_cols, out_span), F32), pltpu.VMEM((n_pairs, own_cols, 128), F32),
                   pltpu.VMEM((2, reach, n_pairs * 128), F32)),
        in_specs=[hbm] * 4,
        out_specs=[vmem] * 3,
        scratch_shapes=[
            pltpu.VMEM((n_rows, n_cols, span), F32),
            pltpu.VMEM((2, n_rows, 8, span), F32),
            pltpu.VMEM((2, n_rows, n_cols), jnp.int32),
            pltpu.VMEM(t_high.shape, BF16),
            pltpu.VMEM(t_low.shape, BF16),
            pltpu.VMEM((2, n_pairs, 1, (n_cols + 32 + 127) // 128 * 128), jnp.int32),
            pltpu.VMEM((n_pairs + 2, padded, width), F32),
            pltpu.VMEM((2, n_pairs + 2, 1, width), F32),
            pltpu.VMEM((2, n_pairs + 2, 1, width), F32),
            pltpu.VMEM((padded, width), F32),
            pltpu.VMEM((2, 1, width), F32),
            pltpu.VMEM((2, reach, n_pairs * 128), F32),
            pltpu.VMEM((2, reach, n_pairs * 128), F32),
            pltpu.SemaphoreType.DMA((n_pairs,)),
            pltpu.SemaphoreType.DMA((2,)),
            pltpu.SemaphoreType.DMA((3,)),
            pltpu.SemaphoreType.DMA((7,)),
            pltpu.SemaphoreType.DMA((7,)),
        ],
        compiler_params=pltpu.CompilerParams(collective_id=0, has_side_effects=True, vmem_limit_bytes=24 * 2**20),
        name="binning",
    )(*[pltpu.with_memory_space_constraint(a, pltpu.HBM) for a in (traces, bin_steps, jnp.asarray(t_high), jnp.asarray(t_low))])
    return pl.pallas_call(
        finish,
        out_shape=jax.ShapeDtypeStruct((n_pairs, own_cols, out_span), F32),
        in_specs=[vmem] * 4,
        out_specs=hbm,
        scratch_shapes=[pltpu.VMEM((n_pairs, own_cols, out_span), F32), pltpu.SemaphoreType.DMA((n_pairs,))],
        compiler_params=pltpu.CompilerParams(vmem_limit_bytes=16 * 2**20),
        name="finish",
    )(main, scale, halo, jnp.asarray(t_edge))


def solution(mesh):
    if mesh.shape["il"] != 2:
        raise ValueError("il size")
    return jax.shard_map(
        functools.partial(shards, mesh.shape["xl"], mesh.shape["ta"]),
        mesh=mesh,
        in_specs=(P("il", "xl", "ta"), P(None, "il", "xl")),
        out_specs=P("il", "xl", "ta"),
        check_vma=False,
    )
```

time: 20.9 us -> 13.2 us (0.63)
  Pallas kernels: 18.3 us -> 13.1 us
  local copies, waits for them, and re-layouts: 2.43 us -> 0.01 us
    pallas_call x1 -> x2, Pallas kernels: 18.3 us -> 13.1 us  [the longest x1 11.4 us: shards(): pl.pallas_call(functools.partial(binning, n_xl, n_ta), out_shape=(pltpu.V...]
    unnamed x1 -> x2, local copies, waits for them, and re-layouts: 2.43 us -> 0.01 us
where the time goes in v2:
time: 13.2 us; the launch traced here: 13.1 us
  Pallas kernels  13.1 us (99%)
    pallas_call x1, Pallas kernels, shards(): pl.pallas_call(functools.partial(binning, n_xl, n_ta), out_shape=(pltpu.V...  11.4 us
    pallas_call x1, Pallas kernels, shards(): pl.pallas_call(finish, out_shape=jax.ShapeDtypeStruct((n_pairs, own_cols,...  1.65 us

profile of v2, /device:TPU:0, one launch (start us, length us, event | category | flops | bytes accessed | tf_op | source)
XLA Modules:
  0.0 13.1 jit_solution(16983719774787270958)
XLA Ops:
  0.0 0.0 copy-start
  0.0 11.4 %binning.1 = (f32[8,104,384]{2,1,0:T(8,128)S(1)}, f32[8,104,128]{2,1,0:T(8,128)S(1)}, f32[2,8,1024]{2,1,0:T(8,128)S(1)}) custom-call(f32[16,208,256]{2,1,0:T(8,128)} %traces.1, s32[2,16,208]{2,1,0:T(8,128)} %steps_hbm.1, bf16[256,384]{1,0:T(8,128)(2,1)} %constant.6.clone.t_high_hbm, bf16[256,384]{1,0:T(8,128)(2,1)} %constant.7.clone.t_low_hbm), custom_call_target="tpu_custom_call" | custom-call | tf_op jit(solution)/shard_map/binning/pallas_call | solution.py:240
  11.4 0.0 copy-done
  11.4 1.7 %finish.1 = f32[8,104,384]{2,1,0:T(8,128)} custom-call(f32[8,104,384]{2,1,0:T(8,128)S(1)} %get-tuple-element.8.main, f32[8,104,128]{2,1,0:T(8,128)S(1)} %get-tuple-element.9.scale, f32[2,8,1024]{2,1,0:T(8,128)S(1)} %get-tuple-element.10.halo, bf16[2,16,384]{2,1,0:T(8,128)(2,1)S(1)} %copy-done), custom_call_target="tpu_custom_call" | custom-call | tf_op jit(solution)/shard_map/finish/pallas_call | solution.py:269
Async XLA Ops:
  0.0 11.4 %copy-start = (bf16[2,16,384]{2,1,0:T(8,128)(2,1)S(1)}, bf16[2,16,384]{2,1,0:T(8,128)(2,1)}, u32[]{:S(2)}) copy-start(bf16[2,16,384]{2,1,0:T(8,128)(2,1)} %constant.8.clone.t_edge) | copy-start | bytes 73732

commit v3 on v2

--- a/solution.py
+++ b/solution.py
@@ -52,8 +52,8 @@
     return ranges
 
 
-def binning(n_xl, n_ta, traces, steps_hbm, t_high_hbm, t_low_hbm, main, scale, halo_out, x, edge_x, steps, t_high, t_low, keys,
-            acc, rim_send, rim_recv, il_recv, corner_recv, halo_send, halo_recv, load_sem, edge_sem, table_sem,
+def binning(n_xl, n_ta, traces, steps_hbm, t_high_hbm, t_low_hbm, main, halo_out, x, edge_x, steps, t_high, t_low, keys,
+            acc, stacked, rim_send, rim_recv, il_recv, corner_recv, halo_send, halo_recv, load_sem, edge_sem, table_sem,
             send_sem, recv_sem):
     n_rows, n_cols, span = x.shape
     n_pairs = n_rows // 2
@@ -81,8 +81,12 @@
     for p in range(n_pairs):
         rows = pl.ds(2 * pair(p), 2)
         loads.append(pltpu.make_async_copy(traces.at[rows], x.at[rows], load_sem.at[p]))
-    for load in loads:
-        load.start()
+
+    def load_pair(p):
+        rows = pl.ds(2 * pair(p), 2)
+        pltpu.make_async_copy(traces.at[rows], x.at[rows], load_sem.at[p]).start()
+
+    pl.loop(0, n_pairs)(load_pair)
     table_loads = [pltpu.make_async_copy(t_high_hbm, t_high, table_sem.at[0]),
                    pltpu.make_async_copy(t_low_hbm, t_low, table_sem.at[1])]
     for load in table_loads:
@@ -154,17 +158,17 @@
         for r in range(n_pairs + 2):
             rim_send[d, r, :, :span] = sums[r: r + 1]
             rim_send[d, r, :, span:] = folds[r: r + 1]
-    bin_pair(0)
     peers = 1
     for d in range(2):
         peers = peers + jnp.where(has_xl[d], 2, 0) + jnp.where(has_ta[d], 1, 0)
     pl.semaphore_wait(barrier, peers)
-    to_other.start()
     for d in range(2):
         def go(d=d):
             for copy in rims[d]:
                 copy.start()
         when(has_xl[d], go)
+    bin_pair(0)
+    to_other.start()
     for p in range(1, n_pairs):
         bin_pair(p)
     to_other.wait_recv()
@@ -181,16 +185,21 @@
     halos = [remote(halo_send.at[d], halo_recv.at[d], 5 + d, {"ta": ta_at[d]}) for d in range(2)]
     for b in range(n_pairs):
         lanes = slice(b * 128, b * 128 + own_cols)
-        halo_send[0, :, lanes] = acc[b + 1, 1: own_cols + 1, span - 128: span].T[128 - reach:]
-        halo_send[1, :, lanes] = acc[b + 1, 1: own_cols + 1, :128].T[:reach]
+        factor = 1.0 / jnp.maximum(acc[b + 1, 1: own_cols + 1, span:], 1.0)
+        for k in range(span // 128):
+            part = acc[b + 1, 1: own_cols + 1, k * 128: (k + 1) * 128] * factor
+            stacked[b, :, k * 128: (k + 1) * 128] = part
+            if k == span // 128 - 1:
+                halo_send[0, :, lanes] = part.T[128 - reach:]
+            if k == 0:
+                halo_send[1, :, lanes] = part.T[:reach]
     for d in range(2):
         when(has_ta[d], halos[d].start)
     for load in table_loads:
         load.wait()
     for b in range(n_pairs):
-        high, low = halves(acc[b + 1, 1: own_cols + 1, :span])
+        high, low = halves(stacked[b])
         main[b] = dot(high, t_high[...]) + (dot(low, t_high[...]) + dot(high, t_low[...]))
-        scale[b] = 1.0 / jnp.maximum(acc[b + 1, 1: own_cols + 1, span:], 1.0)
     for d in range(2):
         def arrived(d=d):
             halos[d].wait_recv()
@@ -209,15 +218,15 @@
     to_other.wait_send()
 
 
-def finish(main, scale, halo, t_edge, out, staged, out_sem):
+def finish(main, halo, t_edge, out, staged, out_sem):
     n_pairs, own_cols, width = main.shape
     writes = []
     for b in range(n_pairs):
         lanes = slice(b * 128, (b + 1) * 128)
-        edges = jnp.concatenate([halo[0, :, lanes], halo[1, :, lanes]], axis=0).T[:own_cols]
-        high, low = halves(edges)
-        edge = dot(high, t_edge[0]) + (dot(low, t_edge[0]) + dot(high, t_edge[1]))
-        staged[b] = (main[b] + edge) * jnp.concatenate([scale[b]] * (width // 128), axis=1)
+        edges = jnp.concatenate([halo[0, :, lanes], halo[1, :, lanes]], axis=0)
+        high = edges.astype(BF16).astype(F32)
+        terms = jnp.concatenate([high, edges - high, high], axis=0).T[:own_cols].astype(BF16)
+        staged[b] = main[b] + dot(terms, t_edge[...])
         write = pltpu.make_async_copy(staged.at[b], out.at[b], out_sem.at[b])
         write.start()
         writes.append(write)
@@ -234,15 +243,15 @@
     out_span = span * P_SIZE // Q
     table = lanczos_table(span)
     t_high, t_low = split_table(table[reach:-reach])
-    t_edge = np.stack(split_table(np.concatenate([table[:reach], table[-reach:]])))
+    edge_high, edge_low = split_table(np.concatenate([table[:reach], table[-reach:]]))
+    t_edge = np.concatenate([edge_high, edge_high, edge_low])
     vmem = pl.BlockSpec(memory_space=pltpu.VMEM)
     hbm = pl.BlockSpec(memory_space=pltpu.HBM)
-    main, scale, halo = pl.pallas_call(
+    main, halo = pl.pallas_call(
         functools.partial(binning, n_xl, n_ta),
-        out_shape=(pltpu.VMEM((n_pairs, own_cols, out_span), F32), pltpu.VMEM((n_pairs, own_cols, 128), F32),
-                   pltpu.VMEM((2, reach, n_pairs * 128), F32)),
+        out_shape=(pltpu.VMEM((n_pairs, own_cols, out_span), F32), pltpu.VMEM((2, reach, n_pairs * 128), F32)),
         in_specs=[hbm] * 4,
-        out_specs=[vmem] * 3,
+        out_specs=[vmem] * 2,
         scratch_shapes=[
             pltpu.VMEM((n_rows, n_cols, span), F32),
             pltpu.VMEM((2, n_rows, 8, span), F32),
@@ -251,6 +260,7 @@
             pltpu.VMEM(t_low.shape, BF16),
             pltpu.VMEM((2, n_pairs, 1, (n_cols + 32 + 127) // 128 * 128), jnp.int32),
             pltpu.VMEM((n_pairs + 2, padded, width), F32),
+            pltpu.VMEM((n_pairs, own_cols, span), F32),
             pltpu.VMEM((2, n_pairs + 2, 1, width), F32),
             pltpu.VMEM((2, n_pairs + 2, 1, width), F32),
             pltpu.VMEM((padded, width), F32),
@@ -269,12 +279,12 @@
     return pl.pallas_call(
         finish,
         out_shape=jax.ShapeDtypeStruct((n_pairs, own_cols, out_span), F32),
-        in_specs=[vmem] * 4,
+        in_specs=[vmem] * 3,
         out_specs=hbm,
         scratch_shapes=[pltpu.VMEM((n_pairs, own_cols, out_span), F32), pltpu.SemaphoreType.DMA((n_pairs,))],
         compiler_params=pltpu.CompilerParams(vmem_limit_bytes=16 * 2**20),
         name="finish",
-    )(main, scale, halo, jnp.asarray(t_edge))
+    )(main, halo, jnp.asarray(t_edge))
 
 
 def solution(mesh):

time: 13.2 us -> 12.1 us (0.917)
  Pallas kernels: 13.1 us -> 11.9 us
    pallas_call x1, Pallas kernels: 11.4 us -> 10.6 us  [shards(): pl.pallas_call(functools.partial(binning, n_xl, n_ta), out_shape=(pltpu.V...]
    pallas_call x1, Pallas kernels: 1.65 us -> 1.35 us  [shards(): pl.pallas_call(finish, out_shape=jax.ShapeDtypeStruct((n_pairs, own_cols,...]
where the time goes in v3:
time: 12.1 us; the launch traced here: 11.9 us
  Pallas kernels  11.9 us (98%)
    pallas_call x1, Pallas kernels, shards(): pl.pallas_call(functools.partial(binning, n_xl, n_ta), out_shape=(pltpu.V...  10.6 us
    pallas_call x1, Pallas kernels, shards(): pl.pallas_call(finish, out_shape=jax.ShapeDtypeStruct((n_pairs, own_cols,...  1.35 us

profile of v3, /device:TPU:0, one launch (start us, length us, event | category | flops | bytes accessed | tf_op | source)
XLA Modules:
  0.0 11.9 jit_solution(5804641571458250858)
XLA Ops:
  0.0 0.0 copy-start
  0.0 10.6 %binning.1 = (f32[8,104,384]{2,1,0:T(8,128)S(1)}, f32[2,8,1024]{2,1,0:T(8,128)S(1)}) custom-call(f32[16,208,256]{2,1,0:T(8,128)} %traces.1, s32[2,16,208]{2,1,0:T(8,128)} %steps_hbm.1, bf16[256,384]{1,0:T(8,128)(2,1)} %constant.6.clone.t_high_hbm, bf16[256,384]{1,0:T(8,128)(2,1)} %constant.7.clone.t_low_hbm), custom_call_target="tpu_custom_call" | custom-call | tf_op jit(solution)/shard_map/binning/pallas_call | solution.py:250
  10.6 0.0 copy-done
  10.6 1.4 %finish.1 = f32[8,104,384]{2,1,0:T(8,128)} custom-call(f32[8,104,384]{2,1,0:T(8,128)S(1)} %get-tuple-element.7.main, f32[2,8,1024]{2,1,0:T(8,128)S(1)} %get-tuple-element.8.halo, bf16[48,384]{1,0:T(8,128)(2,1)S(1)} %copy-done), custom_call_target="tpu_custom_call" | custom-call | tf_op jit(solution)/shard_map/finish/pallas_call | solution.py:279
Async XLA Ops:
  0.0 10.6 %copy-start = (bf16[48,384]{1,0:T(8,128)(2,1)S(1)}, bf16[48,384]{1,0:T(8,128)(2,1)}, u32[]{:S(2)}) copy-start(bf16[48,384]{1,0:T(8,128)(2,1)} %constant.8.clone.t_edge) | copy-start | bytes 110596

commit v4 on v3

--- a/solution.py
+++ b/solution.py
@@ -11,6 +11,7 @@
 TAPS = 16
 P_SIZE = 3
 Q = 2
+AHEAD = 2
 MESH = pl.DeviceIdType.MESH
 F32, BF16 = jnp.float32, jnp.bfloat16
 
@@ -53,7 +54,7 @@
 
 
 def binning(n_xl, n_ta, traces, steps_hbm, t_high_hbm, t_low_hbm, main, halo_out, x, edge_x, steps, t_high, t_low, keys,
-            acc, stacked, rim_send, rim_recv, il_recv, corner_recv, halo_send, halo_recv, load_sem, edge_sem, table_sem,
+            acc, acc_ends, one_hot_low, one_hot_high, rim_send, rim_recv, il_recv, il_recv_ends, corner_recv, halo_send, halo_recv, load_sem, edge_sem, table_sem,
             send_sem, recv_sem):
     n_rows, n_cols, span = x.shape
     n_pairs = n_rows // 2
@@ -106,6 +107,8 @@
         when(has_ta[d], lambda d=d: greet({"ta": ta_at[d]}))
 
     acc[...] = jnp.zeros_like(acc)
+    acc_ends[...] = jnp.zeros_like(acc_ends)
+    one_hots = (one_hot_low, one_hot_high)
     step_load.wait()
     ranges = column_ranges(n_cols)
     col = lax.broadcasted_iota(jnp.int32, (n_rows, n_cols), 1)
@@ -125,16 +128,35 @@
         high, low = halves(values)
         return (dot(chosen, high) + dot(chosen, low), dot(chosen, jnp.ones((values.shape[0], 128), BF16)))
 
-    def bin_pair(p):
+    lane = lax.broadcasted_iota(jnp.int32, (1, 128), 1)
+    is_first, is_last = lane < reach, lane >= 128 - reach
+
+    def pair_values(at, start, stop, samples):
+        return jnp.concatenate([x[2 * at, start:stop, samples], x[2 * at + 1, start:stop, samples]], axis=0)
+
+    def bin_edges(p):
         at = pair(p)
         loads[p].wait()
         for k, (start, stop, first, height) in enumerate(ranges):
-            key = keys[k, at][:, :2 * (stop - start)]
-            values = jnp.concatenate([x[2 * at, start:stop, :], x[2 * at + 1, start:stop, :]], axis=0)
-            sums, folds = totals(one_hot(key, 3 * height), values)
+            chosen = one_hot(keys[k, at][:, :2 * (stop - start)], 3 * height)
+            one_hots[k][at] = chosen
+            values = jnp.where(lane < 64, pair_values(at, start, stop, slice(0, 128)),
+                               pair_values(at, start, stop, slice(span - 128, span)))
+            high = values.astype(BF16)
+            low = jnp.where(is_first | is_last, values - high.astype(F32), 1.0).astype(BF16)
+            sums = dot(chosen, jnp.concatenate([high, low], axis=1))
+            ends = jnp.where(is_first | is_last, sums[:, :128], 0.0) + sums[:, 128:]
             for r in range(3):
-                acc[at + r, first: first + height, :span] += sums[r * height: (r + 1) * height]
-                acc[at + r, first: first + height, span:] += folds[r * height: (r + 1) * height]
+                acc_ends[at + r, first: first + height, :] += ends[r * height: (r + 1) * height]
+
+    def bin_pair(p):
+        at = pair(p)
+        for k, (start, stop, first, height) in enumerate(ranges):
+            chosen = one_hots[k][at]
+            high, low = halves(pair_values(at, start, stop, slice(0, span)))
+            sums = dot(chosen, high) + dot(chosen, low)
+            for r in range(3):
+                acc[at + r, first: first + height, :] += sums[r * height: (r + 1) * height]
 
     def remote(src, dst, slot, partner):
         return pltpu.make_async_remote_copy(src_ref=src, dst_ref=dst, send_sem=send_sem.at[slot],
@@ -143,6 +165,7 @@
     rim_row = jnp.where(il == 0, n_pairs + 1, 0)
     own_row = jnp.where(il == 0, n_pairs, 1)
     to_other = remote(acc.at[rim_row], il_recv, 0, {"il": other})
+    ends_to_other = remote(acc_ends.at[rim_row], il_recv_ends, 7, {"il": other})
     rims = [(remote(rim_send.at[d], rim_recv.at[d], 1 + d, {"xl": xl_at[d]}),
              remote(rim_send.at[d, rim_row], corner_recv.at[d], 3 + d, {"il": other, "xl": xl_at[d]}))
             for d in range(2)]
@@ -157,7 +180,8 @@
         sums, folds = totals(one_hot(key, (n_pairs + 2 + 7) // 8 * 8), edge_x[d].reshape(n_rows * 8, span))
         for r in range(n_pairs + 2):
             rim_send[d, r, :, :span] = sums[r: r + 1]
-            rim_send[d, r, :, span:] = folds[r: r + 1]
+            rim_send[d, r, :, span:] = jnp.where(is_first, sums[r: r + 1, :128], jnp.where(
+                is_last, sums[r: r + 1, span - 128:], folds[r: r + 1]))
     peers = 1
     for d in range(2):
         peers = peers + jnp.where(has_xl[d], 2, 0) + jnp.where(has_ta[d], 1, 0)
@@ -167,38 +191,54 @@
             for copy in rims[d]:
                 copy.start()
         when(has_xl[d], go)
-    bin_pair(0)
-    to_other.start()
+    bin_edges(0)
+    ends_to_other.start()
     for p in range(1, n_pairs):
+        bin_edges(p)
+    for p in range(AHEAD):
         bin_pair(p)
+        if p == 0:
+            to_other.start()
+    ends_to_other.wait_recv()
+    acc_ends[own_row] = acc_ends[own_row] + il_recv_ends[...]
+    for d, column in enumerate((1, own_cols)):
+        def add_ends(d=d, column=column):
+            for copy in rims[d]:
+                copy.wait_recv()
+            for r in range(1, n_pairs + 1):
+                acc_ends[r, column: column + 1, :] += rim_recv[d, r, :, span:]
+            acc_ends[own_row, column: column + 1, :] += corner_recv[d, :, span:]
+        when(has_xl[1 - d], add_ends)
+
+    halos = [remote(halo_send.at[d], halo_recv.at[d], 5 + d, {"ta": ta_at[d]}) for d in range(2)]
+    for b in range(n_pairs):
+        lanes = slice(b * 128, b * 128 + own_cols)
+        ends = acc_ends[b + 1, 1: own_cols + 1, :].T
+        factor = 1.0 / jnp.maximum(ends[64:64 + reach], 1.0)
+        halo_send[0, :, lanes] = ends[128 - reach:] * factor
+        halo_send[1, :, lanes] = ends[:reach] * factor
+    for d in range(2):
+        when(has_ta[d], halos[d].start)
+
+    for p in range(AHEAD, n_pairs):
+        bin_pair(p)
+        if p == 0:
+            to_other.start()
     to_other.wait_recv()
     acc[own_row] = acc[own_row] + il_recv[...]
     for d, column in enumerate((1, own_cols)):
         def add(d=d, column=column):
-            for copy in rims[d]:
-                copy.wait_recv()
             for r in range(1, n_pairs + 1):
-                acc[r, column: column + 1, :] += rim_recv[d, r]
-            acc[own_row, column: column + 1, :] += corner_recv[d]
+                acc[r, column: column + 1, :] += rim_recv[d, r, :, :span]
+            acc[own_row, column: column + 1, :] += corner_recv[d, :, :span]
         when(has_xl[1 - d], add)
-
-    halos = [remote(halo_send.at[d], halo_recv.at[d], 5 + d, {"ta": ta_at[d]}) for d in range(2)]
-    for b in range(n_pairs):
-        lanes = slice(b * 128, b * 128 + own_cols)
-        factor = 1.0 / jnp.maximum(acc[b + 1, 1: own_cols + 1, span:], 1.0)
-        for k in range(span // 128):
-            part = acc[b + 1, 1: own_cols + 1, k * 128: (k + 1) * 128] * factor
-            stacked[b, :, k * 128: (k + 1) * 128] = part
-            if k == span // 128 - 1:
-                halo_send[0, :, lanes] = part.T[128 - reach:]
-            if k == 0:
-                halo_send[1, :, lanes] = part.T[:reach]
-    for d in range(2):
-        when(has_ta[d], halos[d].start)
     for load in table_loads:
         load.wait()
     for b in range(n_pairs):
-        high, low = halves(stacked[b])
+        fold = jnp.broadcast_to(acc_ends[b + 1, 1: own_cols + 1, 64:65], (own_cols, 128))
+        factor = 1.0 / jnp.maximum(fold, 1.0)
+        sums = acc[b + 1, 1: own_cols + 1, :]
+        high, low = halves(sums * jnp.concatenate([factor] * (span // 128), axis=1))
         main[b] = dot(high, t_high[...]) + (dot(low, t_high[...]) + dot(high, t_low[...]))
     for d in range(2):
         def arrived(d=d):
@@ -216,6 +256,7 @@
                 copy.wait_send()
         when(has_xl[d], sent)
     to_other.wait_send()
+    ends_to_other.wait_send()
 
 
 def finish(main, halo, t_edge, out, staged, out_sem):
@@ -259,19 +300,22 @@
             pltpu.VMEM(t_high.shape, BF16),
             pltpu.VMEM(t_low.shape, BF16),
             pltpu.VMEM((2, n_pairs, 1, (n_cols + 32 + 127) // 128 * 128), jnp.int32),
-            pltpu.VMEM((n_pairs + 2, padded, width), F32),
-            pltpu.VMEM((n_pairs, own_cols, span), F32),
+            pltpu.VMEM((n_pairs + 2, padded, span), F32),
+            pltpu.VMEM((n_pairs + 2, padded, 128), F32),
+            *[pltpu.VMEM((n_pairs, 3 * height, 2 * (stop - start)), BF16)
+              for start, stop, _, height in column_ranges(n_cols)],
             pltpu.VMEM((2, n_pairs + 2, 1, width), F32),
             pltpu.VMEM((2, n_pairs + 2, 1, width), F32),
-            pltpu.VMEM((padded, width), F32),
+            pltpu.VMEM((padded, span), F32),
+            pltpu.VMEM((padded, 128), F32),
             pltpu.VMEM((2, 1, width), F32),
             pltpu.VMEM((2, reach, n_pairs * 128), F32),
             pltpu.VMEM((2, reach, n_pairs * 128), F32),
             pltpu.SemaphoreType.DMA((n_pairs,)),
             pltpu.SemaphoreType.DMA((2,)),
             pltpu.SemaphoreType.DMA((3,)),
-            pltpu.SemaphoreType.DMA((7,)),
-            pltpu.SemaphoreType.DMA((7,)),
+            pltpu.SemaphoreType.DMA((8,)),
+            pltpu.SemaphoreType.DMA((8,)),
         ],
         compiler_params=pltpu.CompilerParams(collective_id=0, has_side_effects=True, vmem_limit_bytes=24 * 2**20),
         name="binning",

time: 12.1 us -> 12 us (level)
  no operation moved by 1% of the time
where the time goes in v4:
time: 12 us; the launch traced here: 11.8 us
  Pallas kernels  11.8 us (98%)
    pallas_call x1, Pallas kernels, shards(): pl.pallas_call(functools.partial(binning, n_xl, n_ta), out_shape=(pltpu.V...  10.5 us
    pallas_call x1, Pallas kernels, shards(): pl.pallas_call(finish, out_shape=jax.ShapeDtypeStruct((n_pairs, own_cols,...  1.35 us

profile of v4, /device:TPU:0, one launch (start us, length us, event | category | flops | bytes accessed | tf_op | source)
XLA Modules:
  0.0 11.8 jit_solution(18071527234196784762)
XLA Ops:
  0.0 0.0 copy-start
  0.0 10.5 %binning.1 = (f32[8,104,384]{2,1,0:T(8,128)S(1)}, f32[2,8,1024]{2,1,0:T(8,128)S(1)}) custom-call(f32[16,208,256]{2,1,0:T(8,128)} %traces.1, s32[2,16,208]{2,1,0:T(8,128)} %steps_hbm.1, bf16[256,384]{1,0:T(8,128)(2,1)} %constant.6.clone.t_high_hbm, bf16[256,384]{1,0:T(8,128)(2,1)} %constant.7.clone.t_low_hbm), custom_call_target="tpu_custom_call" | custom-call | tf_op jit(solution)/shard_map/binning/pallas_call | solution.py:291
  10.5 0.0 copy-done
  10.5 1.4 %finish.1 = f32[8,104,384]{2,1,0:T(8,128)} custom-call(f32[8,104,384]{2,1,0:T(8,128)S(1)} %get-tuple-element.7.main, f32[2,8,1024]{2,1,0:T(8,128)S(1)} %get-tuple-element.8.halo, bf16[48,384]{1,0:T(8,128)(2,1)S(1)} %copy-done), custom_call_target="tpu_custom_call" | custom-call | tf_op jit(solution)/shard_map/finish/pallas_call | solution.py:323
Async XLA Ops:
  0.0 10.5 %copy-start = (bf16[48,384]{1,0:T(8,128)(2,1)S(1)}, bf16[48,384]{1,0:T(8,128)(2,1)}, u32[]{:S(2)}) copy-start(bf16[48,384]{1,0:T(8,128)(2,1)} %constant.8.clone.t_edge) | copy-start | bytes 110596

commit v5 on v3

--- a/solution.py
+++ b/solution.py
@@ -220,16 +220,20 @@
 
 def finish(main, halo, t_edge, out, staged, out_sem):
     n_pairs, own_cols, width = main.shape
-    writes = []
+    inner = pl.ds(128, width - 256)
+    writes = [pltpu.make_async_copy(main.at[:, :, inner], out.at[:, :, inner], out_sem.at[n_pairs, 0])]
+    writes[0].start()
     for b in range(n_pairs):
         lanes = slice(b * 128, (b + 1) * 128)
         edges = jnp.concatenate([halo[0, :, lanes], halo[1, :, lanes]], axis=0)
         high = edges.astype(BF16).astype(F32)
         terms = jnp.concatenate([high, edges - high, high], axis=0).T[:own_cols].astype(BF16)
-        staged[b] = main[b] + dot(terms, t_edge[...])
-        write = pltpu.make_async_copy(staged.at[b], out.at[b], out_sem.at[b])
-        write.start()
-        writes.append(write)
+        ends = dot(terms, t_edge[...])
+        for d, start in enumerate((0, width - 128)):
+            staged[b, d] = main[b, :, start: start + 128] + ends[:, d * 128: (d + 1) * 128]
+            write = pltpu.make_async_copy(staged.at[b, d], out.at[b, :, pl.ds(start, 128)], out_sem.at[b, d])
+            write.start()
+            writes.append(write)
     for write in writes:
         write.wait()
 
@@ -245,6 +249,9 @@
     t_high, t_low = split_table(table[reach:-reach])
     edge_high, edge_low = split_table(np.concatenate([table[:reach], table[-reach:]]))
     t_edge = np.concatenate([edge_high, edge_high, edge_low])
+    t_edge = np.concatenate([t_edge[:, :128], t_edge[:, -128:]], axis=1)
+    if out_span < 384:
+        raise ValueError("sample count")
     vmem = pl.BlockSpec(memory_space=pltpu.VMEM)
     hbm = pl.BlockSpec(memory_space=pltpu.HBM)
     main, halo = pl.pallas_call(
@@ -281,7 +288,7 @@
         out_shape=jax.ShapeDtypeStruct((n_pairs, own_cols, out_span), F32),
         in_specs=[vmem] * 3,
         out_specs=hbm,
-        scratch_shapes=[pltpu.VMEM((n_pairs, own_cols, out_span), F32), pltpu.SemaphoreType.DMA((n_pairs,))],
+        scratch_shapes=[pltpu.VMEM((n_pairs, 2, own_cols, 128), F32), pltpu.SemaphoreType.DMA((n_pairs + 1, 2))],
         compiler_params=pltpu.CompilerParams(vmem_limit_bytes=16 * 2**20),
         name="finish",
     )(main, halo, jnp.asarray(t_edge))

time: 12.1 us -> 12 us (level)
  no operation moved by 1% of the time
where the time goes in v5:
time: 12 us; the launch traced here: 11.9 us
  Pallas kernels  11.8 us (98%)
    pallas_call x1, Pallas kernels, shards(): pl.pallas_call(functools.partial(binning, n_xl, n_ta), out_shape=(pltpu.V...  10.6 us
    pallas_call x1, Pallas kernels, shards(): pl.pallas_call(finish, out_shape=jax.ShapeDtypeStruct((n_pairs, own_cols,...  1.28 us

profile of v5, /device:TPU:0, one launch (start us, length us, event | category | flops | bytes accessed | tf_op | source)
XLA Modules:
  0.0 11.9 jit_solution(4924058794465926316)
XLA Ops:
  0.0 0.0 copy-start
  0.0 10.6 %binning.1 = (f32[8,104,384]{2,1,0:T(8,128)S(1)}, f32[2,8,1024]{2,1,0:T(8,128)S(1)}) custom-call(f32[16,208,256]{2,1,0:T(8,128)} %traces.1, s32[2,16,208]{2,1,0:T(8,128)} %steps_hbm.1, bf16[256,384]{1,0:T(8,128)(2,1)} %constant.6.clone.t_high_hbm, bf16[256,384]{1,0:T(8,128)(2,1)} %constant.7.clone.t_low_hbm), custom_call_target="tpu_custom_call" | custom-call | tf_op jit(solution)/shard_map/binning/pallas_call | solution.py:257
  10.6 0.0 copy-done
  10.6 1.3 %finish.1 = f32[8,104,384]{2,1,0:T(8,128)} custom-call(f32[8,104,384]{2,1,0:T(8,128)S(1)} %get-tuple-element.7.main, f32[2,8,1024]{2,1,0:T(8,128)S(1)} %get-tuple-element.8.halo, bf16[48,256]{1,0:T(8,128)(2,1)S(1)} %copy-done), custom_call_target="tpu_custom_call" | custom-call | tf_op jit(solution)/shard_map/finish/pallas_call | solution.py:286
Async XLA Ops:
  0.0 10.6 %copy-start = (bf16[48,256]{1,0:T(8,128)(2,1)S(1)}, bf16[48,256]{1,0:T(8,128)(2,1)}, u32[]{:S(2)}) copy-start(bf16[48,256]{1,0:T(8,128)(2,1)} %constant.8.clone.t_edge) | copy-start | bytes 73732

commit v6 on v4

--- a/solution.py
+++ b/solution.py
@@ -83,6 +83,19 @@
         rows = pl.ds(2 * pair(p), 2)
         loads.append(pltpu.make_async_copy(traces.at[rows], x.at[rows], load_sem.at[p]))
 
+    barrier = pltpu.get_barrier_semaphore()
+
+    def greet(partner):
+        pl.semaphore_signal(barrier, inc=1, device_id=partner, device_id_type=MESH)
+
+    greet({"il": other})
+    for d in range(2):
+        def both(d=d):
+            greet({"xl": xl_at[d]})
+            greet({"il": other, "xl": xl_at[d]})
+        when(has_xl[d], both)
+        when(has_ta[d], lambda d=d: greet({"ta": ta_at[d]}))
+
     def load_pair(p):
         rows = pl.ds(2 * pair(p), 2)
         pltpu.make_async_copy(traces.at[rows], x.at[rows], load_sem.at[p]).start()
@@ -92,19 +105,6 @@
                    pltpu.make_async_copy(t_low_hbm, t_low, table_sem.at[1])]
     for load in table_loads:
         load.start()
-
-    barrier = pltpu.get_barrier_semaphore()
-
-    def greet(partner):
-        pl.semaphore_signal(barrier, inc=1, device_id=partner, device_id_type=MESH)
-
-    greet({"il": other})
-    for d in range(2):
-        def both(d=d):
-            greet({"xl": xl_at[d]})
-            greet({"il": other, "xl": xl_at[d]})
-        when(has_xl[d], both)
-        when(has_ta[d], lambda d=d: greet({"ta": ta_at[d]}))
 
     acc[...] = jnp.zeros_like(acc)
     acc_ends[...] = jnp.zeros_like(acc_ends)
@@ -261,16 +261,20 @@
 
 def finish(main, halo, t_edge, out, staged, out_sem):
     n_pairs, own_cols, width = main.shape
-    writes = []
+    inner = pl.ds(128, width - 256)
+    writes = [pltpu.make_async_copy(main.at[:, :, inner], out.at[:, :, inner], out_sem.at[n_pairs, 0])]
+    writes[0].start()
     for b in range(n_pairs):
         lanes = slice(b * 128, (b + 1) * 128)
         edges = jnp.concatenate([halo[0, :, lanes], halo[1, :, lanes]], axis=0)
         high = edges.astype(BF16).astype(F32)
         terms = jnp.concatenate([high, edges - high, high], axis=0).T[:own_cols].astype(BF16)
-        staged[b] = main[b] + dot(terms, t_edge[...])
-        write = pltpu.make_async_copy(staged.at[b], out.at[b], out_sem.at[b])
-        write.start()
-        writes.append(write)
+        ends = dot(terms, t_edge[...])
+        for d, start in enumerate((0, width - 128)):
+            staged[b, d] = main[b, :, start: start + 128] + ends[:, d * 128: (d + 1) * 128]
+            write = pltpu.make_async_copy(staged.at[b, d], out.at[b, :, pl.ds(start, 128)], out_sem.at[b, d])
+            write.start()
+            writes.append(write)
     for write in writes:
         write.wait()
 
@@ -286,6 +290,9 @@
     t_high, t_low = split_table(table[reach:-reach])
     edge_high, edge_low = split_table(np.concatenate([table[:reach], table[-reach:]]))
     t_edge = np.concatenate([edge_high, edge_high, edge_low])
+    t_edge = np.concatenate([t_edge[:, :128], t_edge[:, -128:]], axis=1)
+    if out_span < 384:
+        raise ValueError("sample count")
     vmem = pl.BlockSpec(memory_space=pltpu.VMEM)
     hbm = pl.BlockSpec(memory_space=pltpu.HBM)
     main, halo = pl.pallas_call(
@@ -325,7 +332,7 @@
         out_shape=jax.ShapeDtypeStruct((n_pairs, own_cols, out_span), F32),
         in_specs=[vmem] * 3,
         out_specs=hbm,
-        scratch_shapes=[pltpu.VMEM((n_pairs, own_cols, out_span), F32), pltpu.SemaphoreType.DMA((n_pairs,))],
+        scratch_shapes=[pltpu.VMEM((n_pairs, 2, own_cols, 128), F32), pltpu.SemaphoreType.DMA((n_pairs + 1, 2))],
         compiler_params=pltpu.CompilerParams(vmem_limit_bytes=16 * 2**20),
         name="finish",
     )(main, halo, jnp.asarray(t_edge))

time: 12 us -> 11.9 us (level)
  no operation moved by 1% of the time
where the time goes in v6:
time: 11.9 us; the launch traced here: 11.7 us
  Pallas kernels  11.7 us (98%)
    pallas_call x1, Pallas kernels, shards(): pl.pallas_call(functools.partial(binning, n_xl, n_ta), out_shape=(pltpu.V...  10.4 us
    pallas_call x1, Pallas kernels, shards(): pl.pallas_call(finish, out_shape=jax.ShapeDtypeStruct((n_pairs, own_cols,...  1.28 us

profile of v6, /device:TPU:0, one launch (start us, length us, event | category | flops | bytes accessed | tf_op | source)
XLA Modules:
  0.0 11.7 jit_solution(2873683139957117509)
XLA Ops:
  0.0 0.0 copy-start
  0.0 10.4 %binning.1 = (f32[8,104,384]{2,1,0:T(8,128)S(1)}, f32[2,8,1024]{2,1,0:T(8,128)S(1)}) custom-call(f32[16,208,256]{2,1,0:T(8,128)} %traces.1, s32[2,16,208]{2,1,0:T(8,128)} %steps_hbm.1, bf16[256,384]{1,0:T(8,128)(2,1)} %constant.6.clone.t_high_hbm, bf16[256,384]{1,0:T(8,128)(2,1)} %constant.7.clone.t_low_hbm), custom_call_target="tpu_custom_call" | custom-call | tf_op jit(solution)/shard_map/binning/pallas_call | solution.py:298
  10.4 0.0 copy-done
  10.4 1.3 %finish.1 = f32[8,104,384]{2,1,0:T(8,128)} custom-call(f32[8,104,384]{2,1,0:T(8,128)S(1)} %get-tuple-element.7.main, f32[2,8,1024]{2,1,0:T(8,128)S(1)} %get-tuple-element.8.halo, bf16[48,256]{1,0:T(8,128)(2,1)S(1)} %copy-done), custom_call_target="tpu_custom_call" | custom-call | tf_op jit(solution)/shard_map/finish/pallas_call | solution.py:330
Async XLA Ops:
  0.0 10.4 %copy-start = (bf16[48,256]{1,0:T(8,128)(2,1)S(1)}, bf16[48,256]{1,0:T(8,128)(2,1)}, u32[]{:S(2)}) copy-start(bf16[48,256]{1,0:T(8,128)(2,1)} %constant.8.clone.t_edge) | copy-start | bytes 73732

commit v7 on v6

--- a/solution.py
+++ b/solution.py
@@ -11,7 +11,7 @@
 TAPS = 16
 P_SIZE = 3
 Q = 2
-AHEAD = 2
+AHEAD = 1
 MESH = pl.DeviceIdType.MESH
 F32, BF16 = jnp.float32, jnp.bfloat16
 

time: 11.9 us -> 11.9 us (level)
  no operation moved by 1% of the time
where the time goes in v7:
time: 11.9 us; the launch traced here: 11.7 us
  Pallas kernels  11.7 us (98%)
    pallas_call x1, Pallas kernels, shards(): pl.pallas_call(functools.partial(binning, n_xl, n_ta), out_shape=(pltpu.V...  10.4 us
    pallas_call x1, Pallas kernels, shards(): pl.pallas_call(finish, out_shape=jax.ShapeDtypeStruct((n_pairs, own_cols,...  1.28 us

profile of v7, /device:TPU:0, one launch (start us, length us, event | category | flops | bytes accessed | tf_op | source)
XLA Modules:
  0.0 11.7 jit_solution(8919942880844252296)
XLA Ops:
  0.0 0.0 copy-start
  0.0 10.4 %binning.1 = (f32[8,104,384]{2,1,0:T(8,128)S(1)}, f32[2,8,1024]{2,1,0:T(8,128)S(1)}) custom-call(f32[16,208,256]{2,1,0:T(8,128)} %traces.1, s32[2,16,208]{2,1,0:T(8,128)} %steps_hbm.1, bf16[256,384]{1,0:T(8,128)(2,1)} %constant.6.clone.t_high_hbm, bf16[256,384]{1,0:T(8,128)(2,1)} %constant.7.clone.t_low_hbm), custom_call_target="tpu_custom_call" | custom-call | tf_op jit(solution)/shard_map/binning/pallas_call | solution.py:298
  10.4 0.0 copy-done
  10.4 1.3 %finish.1 = f32[8,104,384]{2,1,0:T(8,128)} custom-call(f32[8,104,384]{2,1,0:T(8,128)S(1)} %get-tuple-element.7.main, f32[2,8,1024]{2,1,0:T(8,128)S(1)} %get-tuple-element.8.halo, bf16[48,256]{1,0:T(8,128)(2,1)S(1)} %copy-done), custom_call_target="tpu_custom_call" | custom-call | tf_op jit(solution)/shard_map/finish/pallas_call | solution.py:330
Async XLA Ops:
  0.0 10.4 %copy-start = (bf16[48,256]{1,0:T(8,128)(2,1)S(1)}, bf16[48,256]{1,0:T(8,128)(2,1)}, u32[]{:S(2)}) copy-start(bf16[48,256]{1,0:T(8,128)(2,1)} %constant.8.clone.t_edge) | copy-start | bytes 73732
